TPU v7x, 32 devices: a 4x4x1 block of a 4x4x8 slice. The times are simulated.
32 devices in a mesh: dp: 1 (over z), tp: 4 (over y), ep: 8 (over x, core).
Axes of the slice: x: 4, y: 4, z: 1, core: 2. Of those that a mesh axis runs over, the one named last changes fastest.
The devices are a block of a 4x4x8 slice.
Arguments:
- tokens: bfloat16 [32768, 768], P(('dp', 'ep', 'tp'))
- route_ids: int32 [32768, 2], P(('dp', 'ep', 'tp'))
- w_router: bfloat16 [768, 16], replicated
- w_gate: bfloat16 [16, 768, 3072], P('ep', None, 'tp')
- w_up: bfloat16 [16, 768, 3072], P('ep', None, 'tp')
- w_down: bfloat16 [16, 3072, 768], P('ep', 'tp')
- d_out: bfloat16 [32768, 768], P(('dp', 'ep', 'tp'))
Outputs:
- output 1: bfloat16 [32768, 768], P(('dp', 'ep', 'tp'))
- output 2: bfloat16 [32768, 768], P(('dp', 'ep', 'tp'))
- output 3: bfloat16 [16, 768, 3072], P(('dp', 'ep'), None, 'tp')
- output 4: bfloat16 [16, 768, 3072], P(('dp', 'ep'), None, 'tp')
- output 5: bfloat16 [16, 3072, 768], P(('dp', 'ep'), 'tp')
- output 6: float32 [768, 16], P('dp')
All inputs are finite; a program needn't handle non-finite values.
Results may differ from a plain program's by a relative error of at most 0.0124595.
Values are sent between devices in bfloat16 or wider.
A program may use at most 768 MiB of HBM per device.

v0:
```python
import jax
import jax.numpy as jnp
from jax import lax
from jax.sharding import PartitionSpec as P


def route_local(tokens, route_ids, w_router, capacity):
    tok_loc = tokens.shape[0]
    experts = w_router.shape[1]
    expert_ids = jnp.arange(experts)
    logits = jnp.dot(tokens, w_router, preferred_element_type=jnp.float32)
    choice_hot = (route_ids[:, :, None] == expert_ids).astype(jnp.float32)
    chosen = jnp.sum(logits[:, None, :] * choice_hot, axis=2)
    gate_vals = jax.nn.softmax(chosen, axis=1)
    slot_order = (route_ids.T[:, :, None] == expert_ids).astype(jnp.int32).reshape(2 * tok_loc, experts)
    before = jnp.cumsum(slot_order, axis=0) - slot_order
    slot_pos = jnp.sum(before * slot_order, axis=1).reshape(2, tok_loc).T
    slot_hot = (slot_pos[:, :, None] == jnp.arange(capacity)).astype(jnp.bfloat16)
    select = choice_hot.astype(jnp.bfloat16)[:, :, :, None] * slot_hot[:, :, None, :]
    return gate_vals, choice_hot, select.reshape(tok_loc, 2, experts * capacity)


def expert_forward(expert_rows, w_gate, w_up, w_down):
    h_gate = jnp.einsum('erd,edf->erf', expert_rows, w_gate, preferred_element_type=jnp.float32)
    h_up = jnp.einsum('erd,edf->erf', expert_rows, w_up, preferred_element_type=jnp.float32)
    gate_sig = jax.nn.sigmoid(h_gate)
    hidden_act = (h_gate * gate_sig * h_up).astype(jnp.bfloat16)
    part_out = jnp.einsum('erf,efd->erd', hidden_act, w_down, preferred_element_type=jnp.float32).astype(jnp.bfloat16)
    return h_gate, h_up, gate_sig, hidden_act, part_out


def expert_backward(expert_rows, grad_rows, h_gate, h_up, gate_sig, hidden_act, w_gate, w_up, w_down):
    d_act = jnp.einsum('erd,efd->erf', grad_rows, w_down, preferred_element_type=jnp.float32)
    dz_up = (d_act * h_gate * gate_sig).astype(jnp.bfloat16)
    dz_gate = (d_act * h_up * gate_sig * (1.0 + h_gate * (1.0 - gate_sig))).astype(jnp.bfloat16)
    grad_gate = jnp.einsum('erd,erf->edf', expert_rows, dz_gate, preferred_element_type=jnp.float32).astype(jnp.bfloat16)
    grad_up = jnp.einsum('erd,erf->edf', expert_rows, dz_up, preferred_element_type=jnp.float32).astype(jnp.bfloat16)
    grad_down = jnp.einsum('erf,erd->efd', hidden_act, grad_rows, preferred_element_type=jnp.float32).astype(jnp.bfloat16)
    gate_back = jnp.einsum('erf,edf->erd', dz_gate, w_gate, preferred_element_type=jnp.float32)
    up_back = jnp.einsum('erf,edf->erd', dz_up, w_up, preferred_element_type=jnp.float32)
    return grad_gate, grad_up, grad_down, (gate_back + up_back).astype(jnp.bfloat16)


def solution(mesh):
    tp_size = mesh.shape['tp']
    ep_size = mesh.shape['ep']
    tok_spec = P(('dp', 'ep', 'tp'), None)
    in_w_spec = P('ep', None, 'tp')
    down_spec = P('ep', 'tp', None)
    out_w_spec = P(('dp', 'ep'), None, 'tp')
    out_down_spec = P(('dp', 'ep'), 'tp', None)

    def local_step(tokens, route_ids, w_router, w_gate, w_up, w_down, d_out):
        tok_loc, width = tokens.shape
        experts = w_router.shape[1]
        e_loc = w_gate.shape[0]
        capacity = 4 * tok_loc // experts
        gate_vals, choice_hot, select = route_local(tokens, route_ids, w_router, capacity)
        dispatch = jnp.sum(select, axis=1)
        send_rows = jnp.einsum('tm,td->md', dispatch, tokens, preferred_element_type=jnp.float32).astype(jnp.bfloat16).reshape(experts, capacity, width)
        recv_rows = lax.all_to_all(send_rows, 'ep', 0, 1, tiled=True)
        expert_rows = lax.all_gather(recv_rows, 'tp', axis=1, tiled=True)
        h_gate, h_up, gate_sig, hidden_act, part_out = expert_forward(expert_rows, w_gate, w_up, w_down)
        part_back = lax.all_to_all(part_out, 'tp', 1, 0, tiled=True)
        expert_out = jnp.sum(part_back.reshape(tp_size, e_loc, ep_size * capacity, width).astype(jnp.float32), axis=0).astype(jnp.bfloat16)
        home_out = lax.all_to_all(expert_out, 'ep', 1, 0, tiled=True).reshape(experts * capacity, width)
        picked = jnp.einsum('tkm,md->tkd', select, home_out, preferred_element_type=jnp.float32).astype(jnp.bfloat16)
        block_out = jnp.sum(gate_vals[:, :, None] * picked.astype(jnp.float32), axis=1).astype(jnp.bfloat16)

        grad_slot = (gate_vals[:, :, None] * d_out[:, None, :].astype(jnp.float32)).astype(jnp.bfloat16)
        send_grad = jnp.einsum('tkm,tkd->md', select, grad_slot, preferred_element_type=jnp.float32).astype(jnp.bfloat16).reshape(experts, capacity, width)
        d_gates = jnp.einsum('tkd,td->tk', picked, d_out, preferred_element_type=jnp.float32)
        d_chosen = gate_vals * (d_gates - jnp.sum(gate_vals * d_gates, axis=1, keepdims=True))
        d_logits = jnp.sum(d_chosen[:, :, None] * choice_hot, axis=1).astype(jnp.bfloat16)
        grad_router = lax.psum(jnp.einsum('td,te->de', tokens, d_logits, preferred_element_type=jnp.float32), ('ep', 'tp'))
        recv_grad = lax.all_to_all(send_grad, 'ep', 0, 1, tiled=True)
        grad_rows = lax.all_gather(recv_grad, 'tp', axis=1, tiled=True)
        grad_gate, grad_up, grad_down, dx_part = expert_backward(expert_rows, grad_rows, h_gate, h_up, gate_sig, hidden_act, w_gate, w_up, w_down)
        dx_back = lax.all_to_all(dx_part, 'tp', 1, 0, tiled=True)
        expert_dx = jnp.sum(dx_back.reshape(tp_size, e_loc, ep_size * capacity, width).astype(jnp.float32), axis=0).astype(jnp.bfloat16)
        home_dx = lax.all_to_all(expert_dx, 'ep', 1, 0, tiled=True).reshape(experts * capacity, width)
        from_experts = jnp.einsum('tm,md->td', dispatch, home_dx, preferred_element_type=jnp.float32)
        grad_tokens = (from_experts + jnp.einsum('te,de->td', d_logits, w_router, preferred_element_type=jnp.float32)).astype(jnp.bfloat16)
        return block_out, grad_tokens, grad_gate, grad_up, grad_down, grad_router

    return jax.shard_map(local_step, mesh=mesh, in_specs=(tok_spec, tok_spec, P(None, None), in_w_spec, in_w_spec, down_spec, tok_spec), out_specs=(tok_spec, tok_spec, out_w_spec, out_w_spec, out_down_spec, P('dp', None)), check_vma=False)
```

profile of v0, /device:TPU:97, one launch (start us, length us, event | category | flops | bytes accessed | tf_op | source)
XLA Modules:
  0.0 1932.8 jit_solution(9741119788195482999)
XLA Ops:
  9.6 4.5 reduce-window.6
  15.2 12.5 fusion.6
  27.7 7.1 convolution_convert_fusion.1
  34.8 77.1 %all_to_all.90 = bf16[16,256,768]{2,1,0:T(8,128)(2,1)S(1)} all-to-all(bf16[16,256,768]{2,1,0:T(8,128)(2,1)S(1)} %bitcast.107), channel_id=1, replica_groups=mesh['dp'=1,'tp'=4,'ep'=8] {'ep'}, dimensions={0} | all-to-all | bytes 12582912 | tf_op jit(solution)/shard_map/all_to_all | solution.py:61
  115.2 222.6 %all-gather.3.cloned.1.call-done = bf16[2,8192,768]{2,1,0:T(8,128)(2,1)} async-done(((bf16[2,2048,768]{2,1,0:T(8,128)(2,1)}), bf16[2,8192,768]{2,1,0:T(8,128)(2,1)}) %all-gather.3.cloned.1.call-update) | async-done | bytes 25165840 | tf_op jit(solution)/shard_map/all_gather | solution.py:62
  337.8 32.5 %fusion.19 = f32[2,8192,768]{2,1,0:T(8,128)} fusion(bf16[2,8192,768]{2,1,0:T(8,128)(2,1)} %all-gather.3.cloned.1.call-done, bf16[2,768,768]{2,1,0:T(8,128)(2,1)} %param.10), kind=kOutput, calls=%fused_computation.49 | convolution fusion | flops 19327352832 | bytes 77856768 | tf_op jit(solution)/shard_map/erd,edf->erf/dot_general | solution.py:24
  370.3 53.4 %multiply_convert_fusion.2 = (bf16[2,8192,768]{2,1,0:T(8,128)(2,1)}, f32[2,8192,768]{2,1,0:T(8,128)}) fusion(f32[2,8192,768]{2,1,0:T(8,128)} %fusion.19, bf16[2,8192,768]{2,1,0:T(8,128)(2,1)} %all-gather.3.cloned.1.call-done, bf16[2,768,768]{2,1,0:T(8,128)(2,1)} %param.11), kind=kOutput, calls=%fused_computation.3 | convolution fusion | flops 19402850304 | bytes 153354240 | tf_op jit(solution)/shard_map/erd,edf->erf/dot_general | solution.py:25
  423.7 31.9 %convolution_convert_fusion = bf16[2,8192,768]{2,1,0:T(8,128)(2,1)} fusion(bf16[2,8192,768]{2,1,0:T(8,128)(2,1)} %get-tuple-element.12, bf16[2,768,768]{2,1,0:T(8,128)(2,1)S(1)} %copy-done), kind=kOutput, calls=%fused_computation.5 | convolution fusion | flops 19339935744 | bytes 52690944 | tf_op jit(solution)/shard_map/erf,efd->erd/dot_general | solution.py:28
  455.6 44.8 %copy.35 = bf16[2,8192,768]{2,0,1:T(2,128)(2,1)S(1)} copy(bf16[2,8192,768]{2,1,0:T(8,128)(2,1)} %convolution_convert_fusion) | data formatting | bytes 50331648 | tf_op jit(solution)/shard_map/convert_element_type | solution.py:28
  500.4 277.7 %all_to_all.91 = bf16[2,8192,768]{2,0,1:T(2,128)(2,1)} all-to-all(bf16[2,8192,768]{2,0,1:T(2,128)(2,1)S(1)} %copy.35), channel_id=1, replica_groups=mesh['dp'=1,'tp'=4,'ep'=8] {'tp'}, dimensions={1} | all-to-all | bytes 50331648 | tf_op jit(solution)/shard_map/all_to_all | solution.py:64
  778.2 42.9 %reduce_sum.97 = bf16[2,2048,768]{2,0,1:T(2,128)(2,1)} reduce(bf16[2,4,2048,768]{3,0,2,1:T(2,128)(2,1)} %bitcast.91, bf16[]{:T(256)} %constant.17.clone.1), dimensions={1}, to_apply=%region_7.8 | reduce | flops 9437184 | bytes 31457282 | tf_op jit(solution)/shard_map/reduce_sum | solution.py:65
  821.1 6.6 all-to-all-start.2
  833.0 65.8 %all-to-all-done.2 = bf16[2,2048,768]{2,0,1:T(2,128)(2,1)} async-done(((bf16[2,2048,768]{2,0,1:T(2,128)(2,1)}), bf16[2,2048,768]{2,0,1:T(2,128)(2,1)}, u32[]{:S(2)}, u32[]{:S(2)}) %all-to-all-start.2) | async-done | bytes 6291488 | tf_op jit(solution)/shard_map/all_to_all | solution.py:66
  903.0 18.9 convolution_convert_fusion.2
  921.8 8.9 fusion.2
  931.7 17.8 bitcast_convert_fusion
  949.6 74.8 %all_to_all.92 = bf16[16,256,768]{2,1,0:T(8,128)(2,1)S(1)} all-to-all(bf16[16,256,768]{2,1,0:T(8,128)(2,1)S(1)} %bitcast.105), channel_id=1, replica_groups=mesh['dp'=1,'tp'=4,'ep'=8] {'ep'}, dimensions={0} | all-to-all | bytes 12582912 | tf_op jit(solution)/shard_map/all_to_all | solution.py:76
  1027.5 219.1 %all-gather.5.cloned.1.call-done = bf16[2,8192,768]{2,1,0:T(8,128)(2,1)} async-done(((bf16[2,2048,768]{2,1,0:T(8,128)(2,1)}), bf16[2,8192,768]{2,1,0:T(8,128)(2,1)}) %all-gather.5.cloned.1.call-update) | async-done | bytes 25165840 | tf_op jit(solution)/shard_map/all_gather | solution.py:77
  1246.6 68.7 %multiply_convert_fusion = (bf16[2,8192,768]{2,1,0:T(8,128)(2,1)}, bf16[2,8192,768]{2,1,0:T(8,128)(2,1)}) fusion(f32[2,8192,768]{2,1,0:T(8,128)} %fusion.19, f32[2,8192,768]{2,1,0:T(8,128)} %get-tuple-element.13, bf16[2,8192,768]{2,1,0:T(8,128)(2,1)} %all-gather.5.cloned.1.call-done, bf16[2,768,768]{2,1,0:T(8,128)(2,1)S(1)} %copy-done), kind=kOutput, calls=%fused_computation.1 | convolution fusion | flops 19490930688 | bytes 178520064 | tf_op jit(solution)/shard_map/erd,efd->erf/dot_general | solution.py:33
  1315.2 32.7 %fusion.20 = f32[2,8192,768]{2,1,0:T(8,128)} fusion(bf16[2,8192,768]{2,1,0:T(8,128)(2,1)} %get-tuple-element.9, bf16[2,768,768]{2,1,0:T(8,128)(2,1)} %param.10), kind=kOutput, calls=%fused_computation.50 | convolution fusion | flops 19327352832 | bytes 77856768 | tf_op jit(solution)/shard_map/erf,edf->erd/dot_general | solution.py:39
  1348.0 40.1 %add_convert_fusion = bf16[2,8192,768]{2,1,0:T(8,128)(2,1)} fusion(f32[2,8192,768]{2,1,0:T(8,128)} %fusion.20, bf16[2,8192,768]{2,1,0:T(8,128)(2,1)} %get-tuple-element.8, bf16[2,768,768]{2,1,0:T(8,128)(2,1)S(1)} %copy-done.14), kind=kOutput, calls=%fused_computation | convolution fusion | flops 19352518656 | bytes 103022592 | tf_op jit(solution)/shard_map/erf,edf->erd/dot_general | solution.py:40
  1388.0 45.8 %copy.40 = bf16[2,8192,768]{2,0,1:T(2,128)(2,1)} copy(bf16[2,8192,768]{2,1,0:T(8,128)(2,1)} %add_convert_fusion) | data formatting | bytes 50331648 | tf_op jit(solution)/shard_map/convert_element_type | solution.py:41
  1433.9 8.7 all-to-all-start.4
  1442.9 311.6 %psum.7 = f32[768,16]{0,1:T(8,128)} all-reduce(f32[768,16]{0,1:T(8,128)S(1)} %convolution_bitcast_fusion), channel_id=1, replica_groups=mesh['dp'=1,'tp'=4,'ep'=8] {'ep','tp'}, use_global_device_ids=true, to_apply=%region_12.13 | all-reduce | flops 12288 | bytes 98304 | tf_op jit(solution)/shard_map/psum | solution.py:75
  1754.5 4.1 multiply_reduce_fusion
  1758.6 28.4 %convolution_convert_fusion.3 = bf16[2,768,768]{2,1,0:T(8,128)(2,1)} fusion(bf16[2,8192,768]{2,1,0:T(8,128)(2,1)} %get-tuple-element.12, bf16[2,8192,768]{2,1,0:T(8,128)(2,1)} %all-gather.5.cloned.1.call-done), kind=kOutput, calls=%fused_computation.20 | convolution fusion | flops 19328532480 | bytes 52690944 | tf_op jit(solution)/shard_map/erf,erd->efd/dot_general | solution.py:38
  1787.0 42.9 %reduce_sum.99 = bf16[2,2048,768]{2,0,1:T(2,128)(2,1)} reduce(bf16[2,4,2048,768]{3,0,2,1:T(2,128)(2,1)} %bitcast.19, bf16[]{:T(256)} %constant.17.clone.1), dimensions={1}, to_apply=%region_9.10 | reduce | flops 9437184 | bytes 31457282 | tf_op jit(solution)/shard_map/reduce_sum | solution.py:80
  1829.9 5.9 all-to-all-start.5
  1835.8 28.5 %convolution_convert_fusion.4 = bf16[2,768,768]{2,1,0:T(8,128)(2,1)} fusion(bf16[2,8192,768]{2,1,0:T(8,128)(2,1)} %all-gather.3.cloned.1.call-done, bf16[2,8192,768]{2,1,0:T(8,128)(2,1)} %get-tuple-element.8), kind=kOutput, calls=%fused_computation.21 | convolution fusion | flops 19328532480 | bytes 52690944 | tf_op jit(solution)/shard_map/erd,erf->edf/dot_general | solution.py:37
  1864.3 28.6 %convolution_convert_fusion.5 = bf16[2,768,768]{2,1,0:T(8,128)(2,1)} fusion(bf16[2,8192,768]{2,1,0:T(8,128)(2,1)} %all-gather.3.cloned.1.call-done, bf16[2,8192,768]{2,1,0:T(8,128)(2,1)} %get-tuple-element.9), kind=kOutput, calls=%fused_computation.22 | convolution fusion | flops 19328532480 | bytes 52690944 | tf_op jit(solution)/shard_map/erd,erf->edf/dot_general | solution.py:36
  1892.9 13.9 all-to-all-done.5
  1914.6 9.3 fusion.21
  (67 shorter events, 30.2 us)
Async XLA Ops:
  7.2 416.5 %copy-start = (bf16[2,768,768]{2,1,0:T(8,128)(2,1)S(1)}, bf16[2,768,768]{2,1,0:T(8,128)(2,1)}, u32[]{:S(2)}) copy-start(bf16[2,768,768]{2,1,0:T(8,128)(2,1)} %param.12) | copy-start | bytes 7077892
  7.2 330.6 %all-gather.3.cloned.1.call-start = ((), (), s32[]{:S(2)}) async-start(), calls=%async_computation.6 | async-start | bytes 31457280 | tf_op jit(solution)/shard_map/all_gather | solution.py:62
  15.2 12.5 copy-start.3
  27.7 7.1 copy-start.2
  821.1 10.0 copy-start.7
  821.1 11.9 copy-start.5
  821.1 77.7 %all-to-all-start.2 = ((bf16[2,2048,768]{2,0,1:T(2,128)(2,1)}), bf16[2,2048,768]{2,0,1:T(2,128)(2,1)}, u32[]{:S(2)}, u32[]{:S(2)}) async-start(bf16[2,2048,768]{2,0,1:T(2,128)(2,1)} %reduce_sum.97), calls=%async_computation.2 | async-start | bytes 12582912 | tf_op jit(solution)/shard_map/all_to_all | solution.py:66
  827.7 418.9 %all-gather.5.cloned.1.call-start = ((), (), s32[]{:S(2)}) async-start(), calls=%async_computation.7 | async-start | bytes 31457280 | tf_op jit(solution)/shard_map/all_gather | solution.py:77
  931.0 18.5 copy-start.11
  931.7 17.9 copy-start.9
  1315.2 32.7 %copy-start.14 = (bf16[2,768,768]{2,1,0:T(8,128)(2,1)S(1)}, bf16[2,768,768]{2,1,0:T(8,128)(2,1)}, u32[]{:S(2)}) copy-start(bf16[2,768,768]{2,1,0:T(8,128)(2,1)} %param.11) | copy-start | bytes 7077892
  1433.8 8.7 copy-start.10
  1433.8 8.7 copy-start.12
  1433.8 8.7 copy-start.13
  1433.9 8.7 copy-start.6
  1433.9 8.8 copy-start.4
  1433.9 353.1 %all-to-all-start.4 = ((bf16[2,8192,768]{2,0,1:T(2,128)(2,1)}), bf16[2,8192,768]{2,0,1:T(2,128)(2,1)}, u32[]{:S(2)}, u32[]{:S(2)}) async-start(bf16[2,8192,768]{2,0,1:T(2,128)(2,1)} %copy.40), calls=%async_computation.4 | async-start | bytes 50331648 | tf_op jit(solution)/shard_map/all_to_all | solution.py:79
  1829.9 77.0 %all-to-all-start.5 = ((bf16[2,2048,768]{2,0,1:T(2,128)(2,1)}), bf16[2,2048,768]{2,0,1:T(2,128)(2,1)}, u32[]{:S(2)}, u32[]{:S(2)}) async-start(bf16[2,2048,768]{2,0,1:T(2,128)(2,1)} %reduce_sum.99), calls=%async_computation.5 | async-start | bytes 12582912 | tf_op jit(solution)/shard_map/all_to_all | solution.py:81
  1906.8 7.2 slice-start
  1910.6 4.0 slice-start.1
  1914.6 9.4 copy-start.8
  1914.6 11.1 copy-start.1
Sparse Core Ops, SparseCore 0:
  115.3 222.4 all-gather.2
  1027.7 218.8 all-gather.4
where the time goes:
time: 1940 us; the launch traced here: 1930 us
  blocking collectives  741 us (38%)
  waiting for transfers between devices  521 us (27%)
  matrix products  411 us (21%)
  other arithmetic  112 us (6%)
  local copies, waits for them, and re-layouts  111 us (6%)
  starting transfers between devices  21.3 us (1%)
    psum x1, blocking collectives, local_step(): lax.psum(jnp.einsum('td,te->de', tokens, d_logits, preferred_element_type...  312 us
    all_to_all x1, blocking collectives, local_step(): part_back = lax.all_to_all(part_out, 'tp', 1, 0, tiled=True)  278 us
    all_gather x1, waiting for transfers between devices, local_step(): expert_rows = lax.all_gather(recv_rows, 'tp', axis=1, tiled=True)  223 us
    all_gather x1, waiting for transfers between devices, local_step(): grad_rows = lax.all_gather(recv_grad, 'tp', axis=1, tiled=True)  219 us
    all_to_all x1, blocking collectives, local_step(): recv_rows = lax.all_to_all(send_rows, 'ep', 0, 1, tiled=True)  77.1 us
    all_to_all x1, blocking collectives, local_step(): recv_grad = lax.all_to_all(send_grad, 'ep', 0, 1, tiled=True)  74.8 us
    dot_general x1, matrix products, expert_backward(): jnp.einsum('erd,efd->erf', grad_rows, w_down, preferred_element_type=jnp....  68.7 us
    all_to_all x1, waiting for transfers between devices, local_step(): lax.all_to_all(expert_out, 'ep', 1, 0, tiled=True)  65.8 us
  transfers between devices with their start and end apart: 5, of which 4 were waited for; matrix products, arithmetic and copies ran while one was open for 5% of the time, Pallas kernels for 0%

commit v1 on v0

v1 whole, which is shorter than its diff:
```python
import functools
import jax
import jax.numpy as jnp
from jax import lax
from jax.experimental import pallas as pl
from jax.experimental.pallas import tpu as pltpu
from jax.sharding import PartitionSpec as P

F32 = jnp.float32
BF16 = jnp.bfloat16
KEY_STRIDE = 4096
BLOCKS_PER_STEP = 2


def nn(a, b):
    return lax.dot_general(a, b, (((1,), (0,)), ((), ())), preferred_element_type=F32)


def nt(a, b):
    return lax.dot_general(a, b, (((1,), (1,)), ((), ())), preferred_element_type=F32)


def tn(a, b):
    return lax.dot_general(a, b, (((0,), (0,)), ((), ())), preferred_element_type=F32)


def hidden(h1, h3):
    sig = jax.nn.sigmoid(h1)
    return sig, (h1 * sig * h3).astype(BF16)


def hidden_back(da, h1, h3, sig):
    das = da * sig
    dz3 = (das * h1).astype(BF16)
    dz1 = (das * h3 * (1.0 + h1 * (1.0 - sig))).astype(BF16)
    return dz1, dz3


def route_local(tokens, route_ids, w_router):
    experts = w_router.shape[1]
    tok_loc = tokens.shape[0]
    expert_ids = jnp.arange(experts)
    logits = jnp.dot(tokens, w_router, preferred_element_type=F32)
    choice_hot = (route_ids[:, :, None] == expert_ids).astype(F32)
    chosen = jnp.sum(logits[:, None, :] * choice_hot, axis=2)
    gate_vals = jax.nn.softmax(chosen, axis=1)
    slot_order = (route_ids.T[:, :, None] == expert_ids).astype(jnp.int32).reshape(2 * tok_loc, experts)
    before = jnp.cumsum(slot_order, axis=0) - slot_order
    slot_pos = jnp.sum(before * slot_order, axis=1).reshape(2, tok_loc).T
    return gate_vals, slot_pos


def wgrad_kernel(pos_ref, tok_ref, dy_ref, meta_ref, w1_ref, w3_ref, w2_ref,
                 dw1_ref, dw3_ref, dw2_ref, xo_ref, go_ref,
                 acc1, acc3, acc2, xs, gs, az, z1, z3):
    step = pl.program_id(0)
    e_loc, cap = xo_ref.shape[1], xo_ref.shape[2]
    tok_loc, width = tok_ref.shape[1], tok_ref.shape[2]
    cols = w1_ref.shape[2]
    chunk = 256

    @pl.when(step == 0)
    def _():
        acc1[...] = jnp.zeros_like(acc1)
        acc3[...] = jnp.zeros_like(acc3)
        acc2[...] = jnp.zeros_like(acc2)

    tp_size = pos_ref[2]
    slots = lax.broadcasted_iota(jnp.int32, (cap, tok_loc), 0).astype(F32)

    def per_expert(e, carry):
        base = ((pos_ref[0] * e_loc + e) * KEY_STRIDE).astype(F32)
        for b in range(BLOCKS_PER_STEP):
            k0 = meta_ref[b, 0:1, :] - base
            k1 = meta_ref[b, 1:2, :] - base
            use0 = jnp.logical_and(k0 >= 0.0, k0 < float(KEY_STRIDE))
            key = jnp.where(use0, k0, k1)
            gate = jnp.where(use0, meta_ref[b, 2:3, :], meta_ref[b, 3:4, :])
            hit = slots == key
            sel = jnp.where(hit, 1.0, 0.0).astype(BF16)
            g = jnp.sum(jnp.where(hit, gate, 0.0), axis=1, keepdims=True)
            rows = pl.ds(b * cap, cap)
            xs[e, rows, :] = nn(sel, tok_ref[b]).astype(BF16)
            gs[e, rows, :] = (nn(sel, dy_ref[b]) * g).astype(BF16)
        x = xs[e]
        dg = gs[e]
        for c in range(cols // chunk):
            cs = slice(c * chunk, (c + 1) * chunk)
            h1 = nn(x, w1_ref[e, :, cs])
            h3 = nn(x, w3_ref[e, :, cs])
            da = nt(dg, w2_ref[e, cs, :])
            sig, act = hidden(h1, h3)
            dz1, dz3 = hidden_back(da, h1, h3, sig)
            az[:, cs] = act
            z1[:, cs] = dz1
            z3[:, cs] = dz3
        acc1[e] += tn(x, z1[...])
        acc3[e] += tn(x, z3[...])
        acc2[e] += tn(az[...], dg)
        return carry

    lax.fori_loop(0, e_loc, per_expert, 0)

    per_group = tp_size // BLOCKS_PER_STEP
    mine = pos_ref[1]

    @pl.when(lax.rem(step, per_group) == mine // BLOCKS_PER_STEP)
    def _():
        rows = pl.ds(pl.multiple_of(lax.rem(mine, BLOCKS_PER_STEP) * cap, cap), cap)
        xo_ref[0] = xs[:, rows, :]
        go_ref[0] = gs[:, rows, :]

    @pl.when(step == pl.num_programs(0) - 1)
    def _():
        dw1_ref[...] = acc1[...].astype(BF16)
        dw3_ref[...] = acc3[...].astype(BF16)
        dw2_ref[...] = acc2[...].astype(BF16)


def weight_grads(pos, tok_all, dy_all, meta_all, w1, w3, w2, cap, tp_size):
    blocks, tok_loc, width = tok_all.shape
    e_loc, _, cols = w1.shape
    steps = blocks // BLOCKS_PER_STEP
    per_group = tp_size // BLOCKS_PER_STEP
    rows = BLOCKS_PER_STEP * cap
    whole = lambda shape: pl.BlockSpec(shape, lambda i, p: (0,) * len(shape))
    own = pl.BlockSpec((1, e_loc, cap, width), lambda i, p: (i // per_group, 0, 0, 0))
    grid_spec = pltpu.PrefetchScalarGridSpec(
        num_scalar_prefetch=1,
        grid=(steps,),
        in_specs=[
            pl.BlockSpec((BLOCKS_PER_STEP, tok_loc, width), lambda i, p: (i, 0, 0)),
            pl.BlockSpec((BLOCKS_PER_STEP, tok_loc, width), lambda i, p: (i, 0, 0)),
            pl.BlockSpec((BLOCKS_PER_STEP, meta_all.shape[1], tok_loc), lambda i, p: (i, 0, 0)),
            whole(w1.shape), whole(w3.shape), whole(w2.shape),
        ],
        out_specs=[whole(w1.shape), whole(w3.shape), whole(w2.shape), own, own],
        scratch_shapes=[
            pltpu.VMEM(w1.shape, F32), pltpu.VMEM(w3.shape, F32), pltpu.VMEM(w2.shape, F32),
            pltpu.VMEM((e_loc, rows, width), BF16), pltpu.VMEM((e_loc, rows, width), BF16),
            pltpu.VMEM((rows, cols), BF16), pltpu.VMEM((rows, cols), BF16), pltpu.VMEM((rows, cols), BF16),
        ],
    )
    own_shape = jax.ShapeDtypeStruct((blocks // tp_size, e_loc, cap, width), BF16)
    flops = 2 * blocks * e_loc * cap * (6 * width * cols + 2 * tok_loc * width)
    return pl.pallas_call(
        wgrad_kernel,
        grid_spec=grid_spec,
        out_shape=[jax.ShapeDtypeStruct(w.shape, BF16) for w in (w1, w3, w2)] + [own_shape, own_shape],
        compiler_params=pltpu.CompilerParams(dimension_semantics=("arbitrary",), vmem_limit_bytes=62 * 1024 * 1024),
        cost_estimate=pl.CostEstimate(flops=flops, bytes_accessed=4 * tok_all.size, transcendentals=0),
        name="weight_grads",
    )(pos, tok_all, dy_all, meta_all, w1, w3, w2)


def ep_peers(ep_size, me):
    return [lax.rem(me + k, ep_size) for k in range(1, ep_size)]


def rows_kernel(ep_size, tile, x_ref, g_ref, w_ref, home_ref, o_acc, q_acc, send, send_sem, recv_sem, self_sem):
    step = pl.program_id(0)
    steps = ep_size // tile
    me = lax.axis_index('ep')
    cap, width = x_ref.shape[2], x_ref.shape[3]

    @pl.when(step == 0)
    def _():
        barrier = pltpu.get_barrier_semaphore()
        for peer in ep_peers(ep_size, me):
            pl.semaphore_signal(barrier, inc=1, device_id={'ep': peer}, device_id_type=pl.DeviceIdType.MESH)
        pl.semaphore_wait(barrier, ep_size - 1)

    def first_of(at):
        return lax.rem(me // tile + at + 1, steps) * tile

    def remote(slot, dest):
        return pltpu.make_async_remote_copy(
            src_ref=send.at[slot], dst_ref=home_ref.at[me],
            send_sem=send_sem.at[slot], recv_sem=recv_sem.at[me],
            device_id={'ep': dest}, device_id_type=pl.DeviceIdType.MESH)

    @pl.when(step > 0)
    def _():
        for c in range(tile):
            remote((step - 1) * tile + c, first_of(step - 1) + c).start()

    dest = first_of(step)
    x = x_ref[pl.ds(dest, tile), 0].reshape(tile * cap, width)
    dg = g_ref[pl.ds(dest, tile), 0].reshape(tile * cap, width)
    o_acc[...] = jnp.zeros_like(o_acc)
    q_acc[...] = jnp.zeros_like(q_acc)

    def part(j, carry):
        w1 = w_ref[j, 0]
        w3 = w_ref[j, 1]
        w2 = w_ref[j, 2]
        h1 = nn(x, w1)
        h3 = nn(x, w3)
        da = nt(dg, w2)
        sig, act = hidden(h1, h3)
        dz1, dz3 = hidden_back(da, h1, h3, sig)
        o_acc[...] += nn(act, w2).astype(BF16).astype(F32)
        q_acc[...] += (nt(dz1, w1) + nt(dz3, w3)).astype(BF16).astype(F32)
        return carry

    lax.fori_loop(0, w_ref.shape[0], part, 0)
    for c in range(tile):
        rows = slice(c * cap, (c + 1) * cap)
        send[step * tile + c, 0] = o_acc[rows].astype(BF16)
        send[step * tile + c, 1] = q_acc[rows].astype(BF16)

    @pl.when(step == steps - 1)
    def _():
        last = (steps - 1) * tile
        mine = lax.rem(me, tile)
        own = pltpu.make_async_copy(send.at[last + mine], home_ref.at[me], self_sem)
        own.start()
        near = (me // tile) * tile
        for k in range(1, tile):
            c = lax.rem(mine + k, tile)
            remote(last + c, near + c).start()
        for slot in range(last):
            remote(slot, me).wait_send()
        for k in range(1, tile):
            remote(last + lax.rem(mine + k, tile), me).wait_send()
        for peer in ep_peers(ep_size, me):
            pltpu.make_async_remote_copy(
                src_ref=send.at[0], dst_ref=home_ref.at[peer],
                send_sem=send_sem.at[0], recv_sem=recv_sem.at[peer],
                device_id={'ep': peer}, device_id_type=pl.DeviceIdType.MESH).wait_recv()
        own.wait()


def own_rows(xo, go, wg, e, ep_size):
    groups, e_loc, cap, width = xo.shape
    tp_size, _, _, cols = wg.shape
    tile = 2
    in_rows = pl.BlockSpec((groups, 1, cap, width), lambda r: (0, e, 0, 0))
    flops = 12 * groups * cap * width * cols * tp_size
    return pl.pallas_call(
        functools.partial(rows_kernel, ep_size, tile),
        grid=(groups // tile,),
        in_specs=[in_rows, in_rows, pl.BlockSpec(wg.shape, lambda r: (0, 0, 0, 0))],
        out_specs=pl.BlockSpec(memory_space=pl.ANY),
        out_shape=jax.ShapeDtypeStruct((groups, 2, cap, width), BF16),
        scratch_shapes=[
            pltpu.VMEM((tile * cap, width), F32), pltpu.VMEM((tile * cap, width), F32),
            pltpu.VMEM((groups, 2, cap, width), BF16),
            pltpu.SemaphoreType.DMA((groups,)), pltpu.SemaphoreType.DMA((groups,)), pltpu.SemaphoreType.DMA,
        ],
        compiler_params=pltpu.CompilerParams(dimension_semantics=("arbitrary",), vmem_limit_bytes=62 * 1024 * 1024,
                                             collective_id=1 + e, has_side_effects=True),
        cost_estimate=pl.CostEstimate(flops=flops, bytes_accessed=4 * xo.size + 2 * wg.size, transcendentals=0),
        name="own_rows",
    )(xo, go, wg)


def combine_kernel(home0_ref, home1_ref, col_ref, tok_ref, dy_ref, wr_ref, y_ref, du_ref, dwr_ref, p0, p1, px):
    step = pl.program_id(0)
    cap = home0_ref.shape[2]
    tok_loc = tok_ref.shape[0]
    experts = wr_ref.shape[0]

    lane = lax.broadcasted_iota(jnp.int32, (1, 2 * cap), 1)
    target = (step * 2 * KEY_STRIDE + jnp.where(lane >= cap, lane + (KEY_STRIDE - cap), lane)).astype(F32)
    hit0 = col_ref[:, 0:1] == target
    hit1 = col_ref[:, 1:2] == target
    s0 = jnp.where(hit0, 1.0, 0.0).astype(BF16)
    s1 = jnp.where(hit1, 1.0, 0.0).astype(BF16)
    rows_o = jnp.concatenate([home0_ref[0, 0], home1_ref[0, 0]], axis=0)
    rows_x = jnp.concatenate([home0_ref[0, 1], home1_ref[0, 1]], axis=0)

    @pl.when(step == 0)
    def _():
        p0[...] = nn(s0, rows_o)
        p1[...] = nn(s1, rows_o)
        px[...] = nn(s0 + s1, rows_x)

    @pl.when(step > 0)
    def _():
        p0[...] += nn(s0, rows_o)
        p1[...] += nn(s1, rows_o)
        px[...] += nn(s0 + s1, rows_x)

    @pl.when(step == pl.num_programs(0) - 1)
    def _():
        g0 = col_ref[:, 2:3]
        g1 = col_ref[:, 3:4]
        dy = dy_ref[...].astype(F32)
        a0 = p0[...]
        a1 = p1[...]
        y_ref[...] = (g0 * a0 + g1 * a1).astype(BF16)
        d0 = jnp.sum(a0 * dy, axis=1, keepdims=True)
        d1 = jnp.sum(a1 * dy, axis=1, keepdims=True)
        mean = g0 * d0 + g1 * d1
        ids = lax.broadcasted_iota(jnp.int32, (tok_loc, experts), 1).astype(F32)
        dlog = (jnp.where(col_ref[:, 4:5] == ids, g0 * (d0 - mean), 0.0)
                + jnp.where(col_ref[:, 5:6] == ids, g1 * (d1 - mean), 0.0)).astype(BF16)
        du_ref[...] = (px[...] + nn(dlog, wr_ref[...])).astype(BF16)
        dwr_ref[...] = tn(dlog, tok_ref[...])


def combine(home0, home1, cols, tokens, d_out, wr_t):
    groups, _, cap, width = home0.shape
    tok_loc = tokens.shape[0]
    experts = wr_t.shape[0]
    home = pl.BlockSpec((1, 2, cap, width), lambda s: (s, 0, 0, 0))
    whole = lambda a: pl.BlockSpec(a.shape, lambda s: (0,) * a.ndim)
    return pl.pallas_call(
        combine_kernel,
        grid=(groups,),
        in_specs=[home, home, whole(cols), whole(tokens), whole(d_out), whole(wr_t)],
        out_specs=[whole(tokens), whole(tokens), pl.BlockSpec((experts, width), lambda s: (0, 0))],
        out_shape=[jax.ShapeDtypeStruct(tokens.shape, BF16), jax.ShapeDtypeStruct(tokens.shape, BF16),
                   jax.ShapeDtypeStruct((experts, width), F32)],
        scratch_shapes=[pltpu.VMEM(tokens.shape, F32)] * 3,
        compiler_params=pltpu.CompilerParams(dimension_semantics=("arbitrary",), vmem_limit_bytes=62 * 1024 * 1024),
        cost_estimate=pl.CostEstimate(flops=6 * tok_loc * experts * cap * width, bytes_accessed=4 * home0.size, transcendentals=0),
        name="combine",
    )(home0, home1, cols, tokens, d_out, wr_t)


def router_kernel(axes, part_ref, out_ref, buf_a, mid, buf_b, send_a, recv_a, send_b, recv_b):
    sizes = [size for _, size in axes]
    barrier = pltpu.get_barrier_semaphore()
    for name, size in axes:
        me = lax.axis_index(name)
        for k in range(1, size):
            pl.semaphore_signal(barrier, inc=1, device_id={name: lax.rem(me + k, size)}, device_id_type=pl.DeviceIdType.MESH)
    pl.semaphore_wait(barrier, sum(sizes) - len(sizes))

    def exchange(name, size, src, buf, send_sem, recv_sem, out):
        me = lax.axis_index(name)
        copies = []
        for k in range(1, size):
            copy = pltpu.make_async_remote_copy(
                src_ref=src, dst_ref=buf.at[me], send_sem=send_sem.at[k], recv_sem=recv_sem.at[me],
                device_id={name: lax.rem(me + k, size)}, device_id_type=pl.DeviceIdType.MESH)
            copy.start()
            copies.append(copy)
        buf[me] = src[...]
        for k in range(1, size):
            peer = lax.rem(me + k, size)
            pltpu.make_async_remote_copy(
                src_ref=src, dst_ref=buf.at[peer], send_sem=send_sem.at[k], recv_sem=recv_sem.at[peer],
                device_id={name: peer}, device_id_type=pl.DeviceIdType.MESH).wait_recv()
        total = buf[0]
        for k in range(1, size):
            total = total + buf[k]
        out[...] = total
        return copies

    copies = exchange(*axes[0], part_ref, buf_a, send_a, recv_a, mid)
    copies += exchange(*axes[1], mid, buf_b, send_b, recv_b, out_ref)
    for copy in copies:
        copy.wait_send()


def router_sum(part, ep_size, tp_size):
    shape = part.shape
    vmem = pl.BlockSpec(memory_space=pltpu.VMEM)
    return pl.pallas_call(
        functools.partial(router_kernel, (('ep', ep_size), ('tp', tp_size))),
        in_specs=[vmem],
        out_specs=vmem,
        out_shape=jax.ShapeDtypeStruct(shape, F32),
        scratch_shapes=[
            pltpu.VMEM((ep_size,) + shape, F32), pltpu.VMEM(shape, F32), pltpu.VMEM((tp_size,) + shape, F32),
            pltpu.SemaphoreType.DMA((ep_size,)), pltpu.SemaphoreType.DMA((ep_size,)),
            pltpu.SemaphoreType.DMA((tp_size,)), pltpu.SemaphoreType.DMA((tp_size,)),
        ],
        compiler_params=pltpu.CompilerParams(collective_id=3, has_side_effects=True),
        cost_estimate=pl.CostEstimate(flops=12 * part.size, bytes_accessed=8 * part.size, transcendentals=0),
        name="router_sum",
    )(part)


def solution(mesh):
    tp_size = mesh.shape['tp']
    ep_size = mesh.shape['ep']
    tok_spec = P(('dp', 'ep', 'tp'), None)
    in_w_spec = P('ep', None, 'tp')
    down_spec = P('ep', 'tp', None)
    out_w_spec = P(('dp', 'ep'), None, 'tp')
    out_down_spec = P(('dp', 'ep'), 'tp', None)

    def local_step(tokens, route_ids, w_router, w_gate, w_up, w_down, d_out):
        tok_loc, width = tokens.shape
        experts = w_router.shape[1]
        capacity = 4 * tok_loc // experts
        tok_all = lax.all_gather(tokens, ('ep', 'tp'), axis=0, tiled=False)
        dy_all = lax.all_gather(d_out, ('ep', 'tp'), axis=0, tiled=False)
        packed = [jnp.stack([w_gate[e], w_up[e], w_down[e]]) for e in range(w_gate.shape[0])]
        w_all = [lax.all_gather(w, 'tp', axis=0, tiled=False) for w in packed]

        gate_vals, slot_pos = route_local(tokens, route_ids, w_router)
        keys = (route_ids * KEY_STRIDE + slot_pos).astype(F32)
        meta = jnp.concatenate([keys.T, gate_vals.T], axis=0)
        meta_all = lax.all_gather(meta, ('ep', 'tp'), axis=0, tiled=False)

        pos = jnp.stack([lax.axis_index('ep'), lax.axis_index('tp'), jnp.int32(tp_size)]).astype(jnp.int32)
        grad_gate, grad_up, grad_down, xo, go = weight_grads(pos, tok_all, dy_all, meta_all, w_gate, w_up, w_down, capacity, tp_size)
        home0, home1 = [own_rows(xo, go, w_all[e], e, ep_size) for e in range(2)]
        cols = jnp.concatenate([keys, gate_vals, route_ids.astype(F32), jnp.zeros_like(gate_vals)], axis=1)
        block_out, grad_tokens, router_part = combine(home0, home1, cols, tokens, d_out, w_router.T)
        grad_router = router_sum(router_part, ep_size, tp_size).T
        return block_out, grad_tokens, grad_gate, grad_up, grad_down, grad_router

    return jax.shard_map(local_step, mesh=mesh, in_specs=(tok_spec, tok_spec, P(None, None), in_w_spec, in_w_spec, down_spec, tok_spec), out_specs=(tok_spec, tok_spec, out_w_spec, out_w_spec, out_down_spec, P('dp', None)), check_vma=False)
```

time: 1940 us -> 797 us (0.41)
  blocking collectives: 741 us -> 34.3 us
  Pallas kernels: 0 us -> 467 us
  matrix products: 411 us -> 0.5 us
  waiting for transfers between devices: 521 us -> 263 us
  local copies, waits for them, and re-layouts: 111 us -> 6.97 us
  other arithmetic: 112 us -> 9.88 us
  starting transfers between devices: 21.3 us -> 0.25 us
    pallas_call x0 -> x5, Pallas kernels: none -> 467 us  [the longest x2 223 us: own_rows(): pl.pallas_call(functools.partial(rows_kernel, ep_size, tile), grid=(group...]
    all_to_all x3 -> x0, blocking collectives: 430 us -> none  [the longest x1 278 us: local_step(): part_back = lax.all_to_all(part_out, 'tp', 1, 0, tiled=True)]
    dot_general x17 -> x1, matrix products: 411 us -> 0.5 us  [route_local(): logits = jnp.dot(tokens, w_router, preferred_element_type=F32)]
    psum x1 -> x0, blocking collectives: 312 us -> none  [local_step(): lax.psum(jnp.einsum('td,te->de', tokens, d_logits, preferred_element_type...]
    all_gather x2 -> x4, waiting for transfers between devices: 442 us -> 262 us  [the longest x1 153 us: local_step(): dy_all = lax.all_gather(d_out, ('ep', 'tp'), axis=0, tiled=False)]
    reduce_sum x6 -> x0, other arithmetic: 103 us -> none  [the longest x1 42.9 us: local_step(): jnp.sum(part_back.reshape(tp_size, e_loc, ep_size * capacity, width).asty...]
    convert_element_type x2 -> x0, local copies, waits for them, and re-layouts: 90.6 us -> none  [the longest x1 45.8 us: expert_backward(): (gate_back + up_back).astype(jnp.bfloat16)]
    all_to_all x3 -> x0, waiting for transfers between devices: 79.7 us -> none  [the longest x1 65.8 us: local_step(): lax.all_to_all(expert_out, 'ep', 1, 0, tiled=True)]
  transfers between devices with their start and end apart: 5 -> 4, of which waited for: 4 -> 2; matrix products, arithmetic and copies ran while one was open for 5% -> 2% of each run, Pallas kernels for 0% -> 39%
where the time goes in v1:
time: 797 us; the launch traced here: 796 us
  Pallas kernels  467 us (59%)
  waiting for transfers between devices  263 us (33%)
  blocking collectives  34.3 us (4%)
  between operations  14 us (2%)
  other arithmetic  9.88 us (1%)
    pallas_call x2, Pallas kernels, own_rows(): pl.pallas_call(functools.partial(rows_kernel, ep_size, tile), grid=(group...  223 us
    pallas_call x1, Pallas kernels, weight_grads(): pl.pallas_call(wgrad_kernel, grid_spec=grid_spec, out_shape=[jax.ShapeDty...  197 us
    all_gather x1, waiting for transfers between devices, local_step(): dy_all = lax.all_gather(d_out, ('ep', 'tp'), axis=0, tiled=False)  153 us
    all_gather x1, waiting for transfers between devices, local_step(): tok_all = lax.all_gather(tokens, ('ep', 'tp'), axis=0, tiled=False)  108 us
    all_gather x1, blocking collectives, local_step(): meta_all = lax.all_gather(meta, ('ep', 'tp'), axis=0, tiled=False)  34.3 us
    pallas_call x1, Pallas kernels, combine(): pl.pallas_call(combine_kernel, grid=(groups,), in_specs=[home, home, whol...  32.1 us
  transfers between devices with their start and end apart: 4, of which 2 were waited for; matrix products, arithmetic and copies ran while one was open for 2% of the time, Pallas kernels for 39%

profile of v1, /device:TPU:97, one launch (start us, length us, event | category | flops | bytes accessed | tf_op | source)
XLA Modules:
  0.0 796.5 jit_solution(10381953218291436763)
XLA Ops:
  7.2 0.1 all-gather.11.cloned.1.call-start
  7.3 0.7 all-gather.11.cloned.1.call-update
  8.0 0.1 all-gather.13.cloned.1.call-start
  8.1 0.7 all-gather.13.cloned.1.call-update
  8.8 0.1 all-gather.17.cloned.1.call-start
  8.9 0.2 fusion.9
  9.1 1.5 copy-done.2
  10.5 0.7 copy-done.3
  11.3 0.3 fusion.7
  11.6 2.1 pad_maximum_fusion.1
  13.7 0.1 all-gather.15.cloned.1.call-start
  13.8 2.1 pad_maximum_fusion
  15.9 1.3 copy-done
  17.3 0.5 fusion.11
  18.0 4.5 reduce-window.6
  22.5 0.4 slice_reduce_fusion
  23.0 0.2 reduce-window.9
  23.1 0.1 broadcast_add_fusion
  23.3 0.1 fusion.2
  23.4 34.3 %all-gather.5.meta_ref = f32[32,4,1024]{2,1,0:T(4,128)} all-gather(f32[1,4,1024]{2,1,0:T(4,128)S(1)} %maximum_bitcast_fusion), channel_id=4, replica_groups=mesh['dp'=1,'tp'=4,'ep'=8] {'ep','tp'}, dimensions={0}, use_global_device_ids=true | all-gather | bytes 540672 | tf_op jit(solution)/shard_map/all_gather | solution.py:399
  57.7 0.1 pad.3.clone
  57.8 0.1 maximum_maximum_fusion
  57.9 1.0 copy.29.col_ref
  58.9 0.6 pad_add_fusion.pos_ref
  59.5 108.3 %all-gather.11.cloned.1.call-done = bf16[32768,768]{1,0:T(8,128)(2,1)} async-done(((bf16[1024,768]{1,0:T(8,128)(2,1)}), bf16[32768,768]{1,0:T(8,128)(2,1)}) %all-gather.11.cloned.1.call-update) | async-done | bytes 50331664 | tf_op jit(solution)/shard_map/all_gather | solution.py:391
  167.7 153.4 %all-gather.13.cloned.1.call-done = bf16[32768,768]{1,0:T(8,128)(2,1)} async-done(((bf16[1024,768]{1,0:T(8,128)(2,1)}), bf16[32768,768]{1,0:T(8,128)(2,1)}) %all-gather.13.cloned.1.call-update) | async-done | bytes 50331664 | tf_op jit(solution)/shard_map/all_gather | solution.py:392
  321.1 197.3 %weight_grads.1 = (bf16[2,768,768]{2,1,0:T(8,128)(2,1)}, bf16[2,768,768]{2,1,0:T(8,128)(2,1)}, bf16[2,768,768]{2,1,0:T(8,128)(2,1)}, bf16[8,2,256,768]{3,2,1,0:T(8,128)(2,1)}, bf16[8,2,256,768]{3,2,1,0:T(8,128)(2,1)}) custom-call(s32[3]{0:T(128)} %pad_add_fusion.pos_ref, bf16[32,1024,768]{2,1,0:T(8,128)(2,1)} %bitcast.50, bf16[32,1024,768]{2,1,0:T(8,128)(2,1)} %bitcast.51, ...), custom_call_target="tpu_custom_call" | custom-call | flops 167503724544 | bytes 100663296 | tf_op jit(solution)/shard_map/weight_grads/pallas_call | solution.py:146
  518.4 111.7 %own_rows.3.home1_ref = bf16[8,2,256,768]{3,2,1,0:T(8,128)(2,1)} custom-call(bf16[8,2,256,768]{3,2,1,0:T(8,128)(2,1)} %get-tuple-element.14.x_ref, bf16[8,2,256,768]{3,2,1,0:T(8,128)(2,1)} %get-tuple-element.15.g_ref, bf16[4,3,768,768]{3,2,1,0:T(8,128)(2,1)} %bitcast.52), custom_call_target="tpu_custom_call" | custom-call | flops 57982058496 | bytes 26738688 | tf_op jit(solution)/shard_map/own_rows/pallas_call | solution.py:240
  630.1 111.7 %own_rows.2.home0_ref = bf16[8,2,256,768]{3,2,1,0:T(8,128)(2,1)} custom-call(bf16[8,2,256,768]{3,2,1,0:T(8,128)(2,1)} %get-tuple-element.14.x_ref, bf16[8,2,256,768]{3,2,1,0:T(8,128)(2,1)} %get-tuple-element.15.g_ref, bf16[4,3,768,768]{3,2,1,0:T(8,128)(2,1)} %bitcast.53), custom_call_target="tpu_custom_call" | custom-call | flops 57982058496 | bytes 26738688 | tf_op jit(solution)/shard_map/own_rows/pallas_call | solution.py:240
  741.8 32.1 %combine.1 = (bf16[1024,768]{1,0:T(8,128)(2,1)}, bf16[1024,768]{1,0:T(8,128)(2,1)}, f32[16,768]{1,0:T(8,128)}) custom-call(bf16[8,2,256,768]{3,2,1,0:T(8,128)(2,1)} %own_rows.2.home0_ref, bf16[8,2,256,768]{3,2,1,0:T(8,128)(2,1)} %own_rows.3.home1_ref, f32[1024,8]{1,0:T(8,128)} %copy.29.col_ref, bf16[1024,768]{1,0:T(8,128)(2,1)} %tok_ref.1, ...), custom_call_target="tpu_custom_call" | custom-call | flops 19327352832 | bytes 12582912 | tf_op jit(solution)/shard_map/combine/pallas_call | solution.py:309
  773.8 14.7 %router_sum.1 = f32[16,768]{1,0:T(8,128)} custom-call(f32[16,768]{1,0:T(8,128)} %get-tuple-element.21.part_ref), custom_call_target="tpu_custom_call" | custom-call | flops 147456 | bytes 98304 | tf_op jit(solution)/shard_map/router_sum/pallas_call | solution.py:362
  788.5 1.4 copy.36
  (25 shorter events, 0.3 us)
Async XLA Ops:
  7.2 1.7 copy-start.1
  7.2 160.5 %all-gather.11.cloned.1.call-start = ((), (), s32[]{:S(2)}) async-start(), calls=%async_computation | async-start | bytes 51904512 | tf_op jit(solution)/shard_map/all_gather | solution.py:391
  8.0 313.1 %all-gather.13.cloned.1.call-start = ((), (), s32[]{:S(2)}) async-start(), calls=%async_computation.1 | async-start | bytes 51904512 | tf_op jit(solution)/shard_map/all_gather | solution.py:392
  8.8 509.6 %all-gather.17.cloned.1.call-start = ((), (), s32[]{:S(2)}) async-start(), calls=%async_computation.3 | async-start | bytes 17694720 | tf_op jit(solution)/shard_map/all_gather | solution.py:394
  8.9 1.7 copy-start.2
  8.9 2.4 copy-start.3
  13.7 616.4 %all-gather.15.cloned.1.call-start = ((), (), s32[]{:S(2)}) async-start(), calls=%async_computation.2 | async-start | bytes 17694720 | tf_op jit(solution)/shard_map/all_gather | solution.py:394
  15.9 1.4 copy-start
  15.9 1.4 copy-start.5
  15.9 1.9 copy-start.4
Sparse Core Ops, SparseCore 0:
  10.2 157.5 all-gather.10
  169.9 151.2 all-gather.12
  322.7 128.4 all-gather.16
  452.6 130.9 all-gather.14

commit v2 on v1

--- a/solution.py
+++ b/solution.py
@@ -50,13 +50,66 @@
     return gate_vals, slot_pos
 
 
-def wgrad_kernel(pos_ref, tok_ref, dy_ref, meta_ref, w1_ref, w3_ref, w2_ref,
-                 dw1_ref, dw3_ref, dw2_ref, xo_ref, go_ref,
-                 acc1, acc3, acc2, xs, gs, az, z1, z3):
+def choose(pos_ref, meta_ref, b, e, e_loc):
+    base = ((pos_ref[0] * e_loc + e) * KEY_STRIDE).astype(F32)
+    k0 = meta_ref[b, 0:1, :] - base
+    k1 = meta_ref[b, 1:2, :] - base
+    use0 = jnp.logical_and(k0 >= 0.0, k0 < float(KEY_STRIDE))
+    key = jnp.where(use0, k0, k1)
+    gate = jnp.where(use0, meta_ref[b, 2:3, :], meta_ref[b, 3:4, :])
+    return key, gate
+
+
+def hidden_kernel(pos_ref, tok_ref, meta_ref, w1_ref, w3_ref, xs_ref, h1_ref, h3_ref):
+    e_loc = w1_ref.shape[0]
+    tok_loc = tok_ref.shape[1]
+    cap = xs_ref.shape[2] // BLOCKS_PER_STEP
+    slots = lax.broadcasted_iota(jnp.int32, (cap, tok_loc), 0).astype(F32)
+
+    def per_expert(e, carry):
+        for b in range(BLOCKS_PER_STEP):
+            key, _ = choose(pos_ref, meta_ref, b, e, e_loc)
+            sel = jnp.where(slots == key, 1.0, 0.0).astype(BF16)
+            xs_ref[0, e, pl.ds(b * cap, cap), :] = nn(sel, tok_ref[b]).astype(BF16)
+        x = xs_ref[0, e]
+        h1_ref[0, e] = nn(x, w1_ref[e])
+        h3_ref[0, e] = nn(x, w3_ref[e])
+        return carry
+
+    lax.fori_loop(0, e_loc, per_expert, 0)
+
+
+def hidden_rows(pos, tok_all, meta_all, w1, w3, cap):
+    blocks, tok_loc, width = tok_all.shape
+    e_loc, _, cols = w1.shape
+    steps = blocks // BLOCKS_PER_STEP
+    rows = BLOCKS_PER_STEP * cap
+    whole = lambda shape: pl.BlockSpec(shape, lambda i, p: (0,) * len(shape))
+    out = lambda n: pl.BlockSpec((1, e_loc, rows, n), lambda i, p: (i, 0, 0, 0))
+    return pl.pallas_call(
+        hidden_kernel,
+        grid_spec=pltpu.PrefetchScalarGridSpec(
+            num_scalar_prefetch=1, grid=(steps,),
+            in_specs=[pl.BlockSpec((BLOCKS_PER_STEP, tok_loc, width), lambda i, p: (i, 0, 0)),
+                      pl.BlockSpec((BLOCKS_PER_STEP, meta_all.shape[1], tok_loc), lambda i, p: (i, 0, 0)),
+                      whole(w1.shape), whole(w3.shape)],
+            out_specs=[out(width), out(cols), out(cols)]),
+        out_shape=[jax.ShapeDtypeStruct((steps, e_loc, rows, width), BF16),
+                   jax.ShapeDtypeStruct((steps, e_loc, rows, cols), F32),
+                   jax.ShapeDtypeStruct((steps, e_loc, rows, cols), F32)],
+        compiler_params=pltpu.CompilerParams(dimension_semantics=("arbitrary",), vmem_limit_bytes=62 * 1024 * 1024),
+        cost_estimate=pl.CostEstimate(flops=2 * blocks * e_loc * cap * (2 * width * cols + tok_loc * width),
+                                      bytes_accessed=2 * tok_all.size + 8 * steps * e_loc * rows * cols, transcendentals=0),
+        name="hidden_rows",
+    )(pos, tok_all, meta_all, w1, w3)
+
+
+def wgrad_kernel(pos_ref, dy_ref, meta_ref, xs_ref, h1_ref, h3_ref, w2_ref,
+                 dw1_ref, dw3_ref, dw2_ref, xo_ref, go_ref, acc1, acc3, acc2, gs, az, z1, z3):
     step = pl.program_id(0)
     e_loc, cap = xo_ref.shape[1], xo_ref.shape[2]
-    tok_loc, width = tok_ref.shape[1], tok_ref.shape[2]
-    cols = w1_ref.shape[2]
+    tok_loc = dy_ref.shape[1]
+    cols = h1_ref.shape[3]
     chunk = 256
 
     @pl.when(step == 0)
@@ -69,25 +122,18 @@
     slots = lax.broadcasted_iota(jnp.int32, (cap, tok_loc), 0).astype(F32)
 
     def per_expert(e, carry):
-        base = ((pos_ref[0] * e_loc + e) * KEY_STRIDE).astype(F32)
         for b in range(BLOCKS_PER_STEP):
-            k0 = meta_ref[b, 0:1, :] - base
-            k1 = meta_ref[b, 1:2, :] - base
-            use0 = jnp.logical_and(k0 >= 0.0, k0 < float(KEY_STRIDE))
-            key = jnp.where(use0, k0, k1)
-            gate = jnp.where(use0, meta_ref[b, 2:3, :], meta_ref[b, 3:4, :])
+            key, gate = choose(pos_ref, meta_ref, b, e, e_loc)
             hit = slots == key
             sel = jnp.where(hit, 1.0, 0.0).astype(BF16)
             g = jnp.sum(jnp.where(hit, gate, 0.0), axis=1, keepdims=True)
-            rows = pl.ds(b * cap, cap)
-            xs[e, rows, :] = nn(sel, tok_ref[b]).astype(BF16)
-            gs[e, rows, :] = (nn(sel, dy_ref[b]) * g).astype(BF16)
-        x = xs[e]
+            gs[e, pl.ds(b * cap, cap), :] = (nn(sel, dy_ref[b]) * g).astype(BF16)
+        x = xs_ref[0, e]
         dg = gs[e]
         for c in range(cols // chunk):
             cs = slice(c * chunk, (c + 1) * chunk)
-            h1 = nn(x, w1_ref[e, :, cs])
-            h3 = nn(x, w3_ref[e, :, cs])
+            h1 = h1_ref[0, e, :, cs]
+            h3 = h3_ref[0, e, :, cs]
             da = nt(dg, w2_ref[e, cs, :])
             sig, act = hidden(h1, h3)
             dz1, dz3 = hidden_back(da, h1, h3, sig)
@@ -107,7 +153,7 @@
     @pl.when(lax.rem(step, per_group) == mine // BLOCKS_PER_STEP)
     def _():
         rows = pl.ds(pl.multiple_of(lax.rem(mine, BLOCKS_PER_STEP) * cap, cap), cap)
-        xo_ref[0] = xs[:, rows, :]
+        xo_ref[0] = xs_ref[0, :, rows, :]
         go_ref[0] = gs[:, rows, :]
 
     @pl.when(step == pl.num_programs(0) - 1)
@@ -117,80 +163,120 @@
         dw2_ref[...] = acc2[...].astype(BF16)
 
 
-def weight_grads(pos, tok_all, dy_all, meta_all, w1, w3, w2, cap, tp_size):
-    blocks, tok_loc, width = tok_all.shape
+def weight_grads(pos, dy_all, meta_all, xs, h1, h3, w1, w3, w2, cap, tp_size):
+    blocks, tok_loc, width = dy_all.shape
     e_loc, _, cols = w1.shape
     steps = blocks // BLOCKS_PER_STEP
     per_group = tp_size // BLOCKS_PER_STEP
     rows = BLOCKS_PER_STEP * cap
-    whole = lambda shape: pl.BlockSpec(shape, lambda i, p: (0,) * len(shape))
+    whole = lambda shape, **kw: pl.BlockSpec(shape, lambda i, p: (0,) * len(shape), **kw)
     own = pl.BlockSpec((1, e_loc, cap, width), lambda i, p: (i // per_group, 0, 0, 0))
+    tile = lambda a: pl.BlockSpec((1,) + a.shape[1:], lambda i, p: (i, 0, 0, 0))
     grid_spec = pltpu.PrefetchScalarGridSpec(
         num_scalar_prefetch=1,
         grid=(steps,),
         in_specs=[
             pl.BlockSpec((BLOCKS_PER_STEP, tok_loc, width), lambda i, p: (i, 0, 0)),
-            pl.BlockSpec((BLOCKS_PER_STEP, tok_loc, width), lambda i, p: (i, 0, 0)),
             pl.BlockSpec((BLOCKS_PER_STEP, meta_all.shape[1], tok_loc), lambda i, p: (i, 0, 0)),
-            whole(w1.shape), whole(w3.shape), whole(w2.shape),
+            tile(xs), tile(h1), tile(h3), whole(w2.shape, pipeline_mode=pl.Buffered(1)),
         ],
         out_specs=[whole(w1.shape), whole(w3.shape), whole(w2.shape), own, own],
         scratch_shapes=[
             pltpu.VMEM(w1.shape, F32), pltpu.VMEM(w3.shape, F32), pltpu.VMEM(w2.shape, F32),
-            pltpu.VMEM((e_loc, rows, width), BF16), pltpu.VMEM((e_loc, rows, width), BF16),
+            pltpu.VMEM((e_loc, rows, width), BF16),
             pltpu.VMEM((rows, cols), BF16), pltpu.VMEM((rows, cols), BF16), pltpu.VMEM((rows, cols), BF16),
         ],
     )
     own_shape = jax.ShapeDtypeStruct((blocks // tp_size, e_loc, cap, width), BF16)
-    flops = 2 * blocks * e_loc * cap * (6 * width * cols + 2 * tok_loc * width)
+    flops = 2 * blocks * e_loc * cap * (4 * width * cols + tok_loc * width)
     return pl.pallas_call(
         wgrad_kernel,
         grid_spec=grid_spec,
         out_shape=[jax.ShapeDtypeStruct(w.shape, BF16) for w in (w1, w3, w2)] + [own_shape, own_shape],
-        compiler_params=pltpu.CompilerParams(dimension_semantics=("arbitrary",), vmem_limit_bytes=62 * 1024 * 1024),
-        cost_estimate=pl.CostEstimate(flops=flops, bytes_accessed=4 * tok_all.size, transcendentals=0),
+        compiler_params=pltpu.CompilerParams(dimension_semantics=("arbitrary",), vmem_limit_bytes=63 * 1024 * 1024),
+        cost_estimate=pl.CostEstimate(flops=flops, bytes_accessed=2 * dy_all.size + 8 * h1.size, transcendentals=0),
         name="weight_grads",
-    )(pos, tok_all, dy_all, meta_all, w1, w3, w2)
+    )(pos, dy_all, meta_all, xs, h1, h3, w2)
 
 
 def ep_peers(ep_size, me):
     return [lax.rem(me + k, ep_size) for k in range(1, ep_size)]
 
 
-def rows_kernel(ep_size, tile, x_ref, g_ref, w_ref, home_ref, o_acc, q_acc, send, send_sem, recv_sem, self_sem):
+def rows_kernel(ep_size, tile, x_ref, g_ref, w_hbm, home_ref, o_acc, q_acc, w_ref, send, relay,
+                w_sem, send_sem, recv_sem, relay_send, relay_recv, forward_sem, self_sem):
     step = pl.program_id(0)
     steps = ep_size // tile
     me = lax.axis_index('ep')
+    chip = me // tile
+    mine = lax.rem(me, tile)
     cap, width = x_ref.shape[2], x_ref.shape[3]
 
+    def weights(j):
+        return pltpu.make_async_copy(w_hbm.at[j], w_ref.at[j], w_sem.at[j])
+
     @pl.when(step == 0)
     def _():
+        for j in range(w_ref.shape[0]):
+            weights(j).start()
         barrier = pltpu.get_barrier_semaphore()
         for peer in ep_peers(ep_size, me):
             pl.semaphore_signal(barrier, inc=1, device_id={'ep': peer}, device_id_type=pl.DeviceIdType.MESH)
         pl.semaphore_wait(barrier, ep_size - 1)
 
-    def first_of(at):
-        return lax.rem(me // tile + at + 1, steps) * tile
-
-    def remote(slot, dest):
+    def hop(at):
+        return (2 + 3 * at + 3 * (at // 2) + 2 * (at // 3)) % 4
+
+    def chip_at(offset):
+        return lax.rem(chip + offset, steps) * tile
+
+    def push(src, dst, send_at, recv_at, dest):
         return pltpu.make_async_remote_copy(
-            src_ref=send.at[slot], dst_ref=home_ref.at[me],
-            send_sem=send_sem.at[slot], recv_sem=recv_sem.at[me],
+            src_ref=src, dst_ref=dst, send_sem=send_at, recv_sem=recv_at,
             device_id={'ep': dest}, device_id_type=pl.DeviceIdType.MESH)
 
-    @pl.when(step > 0)
+    def direct(slot, src_dev, dest):
+        return push(send.at[slot], home_ref.at[src_dev], send_sem.at[slot], recv_sem.at[src_dev, 0], dest)
+
+    def via(part, c):
+        near = chip_at(1 if part == 0 else steps - 1) + mine
+        return push(send.at[c, part], relay.at[part, c], relay_send.at[part, c], relay_recv.at[part, c], near)
+
+    def forward(part, c):
+        source = chip_at(steps - 1 if part == 0 else 1) + mine
+        dest = chip_at(1 if part == 0 else steps - 1) + c
+        return push(relay.at[part, c], home_ref.at[source, part], forward_sem.at[part, c], recv_sem.at[source, part], dest)
+
+    @pl.when(step == 1)
     def _():
         for c in range(tile):
-            remote((step - 1) * tile + c, first_of(step - 1) + c).start()
-
-    dest = first_of(step)
+            for part in range(2):
+                via(part, c).start()
+
+    @pl.when(step == 2)
+    def _():
+        for c in range(tile):
+            for part in range(2):
+                via(part, c).wait_recv()
+                forward(part, c).start()
+
+    for at in (1, 2):
+        @pl.when(step == at + 1)
+        def _(at=at):
+            for c in range(tile):
+                direct(at * tile + c, me, chip_at(hop(at)) + c).start()
+
+    dest = lax.rem(chip + (2 + 3 * step + 3 * (step // 2) + 2 * (step // 3)), steps) * tile
     x = x_ref[pl.ds(dest, tile), 0].reshape(tile * cap, width)
     dg = g_ref[pl.ds(dest, tile), 0].reshape(tile * cap, width)
     o_acc[...] = jnp.zeros_like(o_acc)
     q_acc[...] = jnp.zeros_like(q_acc)
 
     def part(j, carry):
+        @pl.when(step == 0)
+        def _():
+            weights(j).wait()
+
         w1 = w_ref[j, 0]
         w3 = w_ref[j, 1]
         w2 = w_ref[j, 2]
@@ -212,22 +298,30 @@
     @pl.when(step == steps - 1)
     def _():
         last = (steps - 1) * tile
-        mine = lax.rem(me, tile)
         own = pltpu.make_async_copy(send.at[last + mine], home_ref.at[me], self_sem)
         own.start()
-        near = (me // tile) * tile
+        near = chip * tile
         for k in range(1, tile):
             c = lax.rem(mine + k, tile)
-            remote(last + c, near + c).start()
-        for slot in range(last):
-            remote(slot, me).wait_send()
+            direct(last + c, me, near + c).start()
+        for c in range(tile):
+            for part in range(2):
+                via(part, c).wait_send()
+                forward(part, c).wait_send()
+        for slot in range(tile, last):
+            direct(slot, me, me).wait_send()
         for k in range(1, tile):
-            remote(last + lax.rem(mine + k, tile), me).wait_send()
-        for peer in ep_peers(ep_size, me):
-            pltpu.make_async_remote_copy(
-                src_ref=send.at[0], dst_ref=home_ref.at[peer],
-                send_sem=send_sem.at[0], recv_sem=recv_sem.at[peer],
-                device_id={'ep': peer}, device_id_type=pl.DeviceIdType.MESH).wait_recv()
+            direct(last + lax.rem(mine + k, tile), me, me).wait_send()
+        for offset in range(steps):
+            for k in range(tile):
+                if offset == 0 and k == 0:
+                    continue
+                peer = chip_at(offset) + lax.rem(mine + k, tile)
+                if offset == 2:
+                    for part in range(2):
+                        push(relay.at[part, 0], home_ref.at[peer, part], forward_sem.at[part, 0], recv_sem.at[peer, part], peer).wait_recv()
+                else:
+                    direct(0, peer, peer).wait_recv()
         own.wait()
 
 
@@ -240,13 +334,18 @@
     return pl.pallas_call(
         functools.partial(rows_kernel, ep_size, tile),
         grid=(groups // tile,),
-        in_specs=[in_rows, in_rows, pl.BlockSpec(wg.shape, lambda r: (0, 0, 0, 0))],
+        in_specs=[in_rows, in_rows, pl.BlockSpec(memory_space=pl.ANY)],
         out_specs=pl.BlockSpec(memory_space=pl.ANY),
         out_shape=jax.ShapeDtypeStruct((groups, 2, cap, width), BF16),
         scratch_shapes=[
             pltpu.VMEM((tile * cap, width), F32), pltpu.VMEM((tile * cap, width), F32),
+            pltpu.VMEM(wg.shape, BF16),
             pltpu.VMEM((groups, 2, cap, width), BF16),
-            pltpu.SemaphoreType.DMA((groups,)), pltpu.SemaphoreType.DMA((groups,)), pltpu.SemaphoreType.DMA,
+            pltpu.VMEM((2, tile, cap, width), BF16),
+            pltpu.SemaphoreType.DMA((tp_size,)),
+            pltpu.SemaphoreType.DMA((groups,)), pltpu.SemaphoreType.DMA((groups, 2)),
+            pltpu.SemaphoreType.DMA((2, tile)), pltpu.SemaphoreType.DMA((2, tile)), pltpu.SemaphoreType.DMA((2, tile)),
+            pltpu.SemaphoreType.DMA,
         ],
         compiler_params=pltpu.CompilerParams(dimension_semantics=("arbitrary",), vmem_limit_bytes=62 * 1024 * 1024,
                                              collective_id=1 + e, has_side_effects=True),
@@ -399,7 +498,8 @@
         meta_all = lax.all_gather(meta, ('ep', 'tp'), axis=0, tiled=False)
 
         pos = jnp.stack([lax.axis_index('ep'), lax.axis_index('tp'), jnp.int32(tp_size)]).astype(jnp.int32)
-        grad_gate, grad_up, grad_down, xo, go = weight_grads(pos, tok_all, dy_all, meta_all, w_gate, w_up, w_down, capacity, tp_size)
+        xs, h1, h3 = hidden_rows(pos, tok_all, meta_all, w_gate, w_up, capacity)
+        grad_gate, grad_up, grad_down, xo, go = weight_grads(pos, dy_all, meta_all, xs, h1, h3, w_gate, w_up, w_down, capacity, tp_size)
         home0, home1 = [own_rows(xo, go, w_all[e], e, ep_size) for e in range(2)]
         cols = jnp.concatenate([keys, gate_vals, route_ids.astype(F32), jnp.zeros_like(gate_vals)], axis=1)
         block_out, grad_tokens, router_part = combine(home0, home1, cols, tokens, d_out, w_router.T)

time: 797 us -> 733 us (0.920)
  waiting for transfers between devices: 263 us -> 222 us
  Pallas kernels: 467 us -> 445 us
    pallas_call x0 -> x1, Pallas kernels: none -> 78.7 us  [hidden_rows(): pl.pallas_call(hidden_kernel, grid_spec=pltpu.PrefetchScalarGridSpec(num_...]
    all_gather x1, waiting for transfers between devices: 153 us -> 74.7 us  [local_step(): dy_all = lax.all_gather(d_out, ('ep', 'tp'), axis=0, tiled=False)]
    pallas_call x1, Pallas kernels: 197 us -> 132 us  [weight_grads(): pl.pallas_call(wgrad_kernel, grid_spec=grid_spec, out_shape=[jax.ShapeDty...]
    all_gather x2, waiting for transfers between devices: 0.02 us -> 37.3 us  [local_step(): w_all = [lax.all_gather(w, 'tp', axis=0, tiled=False) for w in packed]]
    pallas_call x2, Pallas kernels: 223 us -> 187 us  [own_rows(): pl.pallas_call(functools.partial(rows_kernel, ep_size, tile), grid=(group...]
  transfers between devices with their start and end apart: 4 -> 4, of which waited for: 2 -> 3; matrix products, arithmetic and copies ran while one was open for 2% -> 2% of each run, Pallas kernels for 39% -> 41%
where the time goes in v2:
time: 733 us
  Pallas kernels  445 us (61%)
  waiting for transfers between devices  222 us (30%)
  blocking collectives  34.4 us (5%)
  between operations  14 us (2%)
  other arithmetic  9.76 us (1%)
    pallas_call x2, Pallas kernels, own_rows(): pl.pallas_call(functools.partial(rows_kernel, ep_size, tile), grid=(group...  187 us
    pallas_call x1, Pallas kernels, weight_grads(): pl.pallas_call(wgrad_kernel, grid_spec=grid_spec, out_shape=[jax.ShapeDty...  132 us
    all_gather x1, waiting for transfers between devices, local_step(): tok_all = lax.all_gather(tokens, ('ep', 'tp'), axis=0, tiled=False)  108 us
    pallas_call x1, Pallas kernels, hidden_rows(): pl.pallas_call(hidden_kernel, grid_spec=pltpu.PrefetchScalarGridSpec(num_...  78.7 us
    all_gather x1, waiting for transfers between devices, local_step(): dy_all = lax.all_gather(d_out, ('ep', 'tp'), axis=0, tiled=False)  74.7 us
    all_gather x2, waiting for transfers between devices, local_step(): w_all = [lax.all_gather(w, 'tp', axis=0, tiled=False) for w in packed]  37.3 us
    all_gather x1, blocking collectives, local_step(): meta_all = lax.all_gather(meta, ('ep', 'tp'), axis=0, tiled=False)  34.4 us
    pallas_call x1, Pallas kernels, combine(): pl.pallas_call(combine_kernel, grid=(groups,), in_specs=[home, home, whol...  32 us
  transfers between devices with their start and end apart: 4, of which 3 were waited for; matrix products, arithmetic and copies ran while one was open for 2% of the time, Pallas kernels for 41%

profile of v2, /device:TPU:97, one launch (start us, length us, event | category | flops | bytes accessed | tf_op | source)
XLA Modules:
  0.0 732.7 jit_solution(5710413827404842758)
XLA Ops:
  7.3 0.7 all-gather.13.cloned.1.call-update
  8.1 0.7 all-gather.11.cloned.1.call-update
  8.8 0.1 all-gather.17.cloned.1.call-start
  8.9 0.2 fusion.9
  9.1 1.5 copy-done.2
  10.5 0.7 copy-done.3
  11.3 0.3 fusion.7
  11.6 2.0 pad_maximum_fusion.1
  13.7 0.1 all-gather.15.cloned.1.call-start
  13.7 2.0 pad_maximum_fusion
  15.8 1.3 copy-done
  17.2 0.5 fusion.11
  17.9 4.5 reduce-window.6
  22.4 0.4 slice_reduce_fusion
  22.8 0.2 reduce-window.9
  23.0 0.1 broadcast_add_fusion
  23.1 0.1 fusion.2
  23.3 34.4 %all-gather.5.meta_ref = f32[32,4,1024]{2,1,0:T(4,128)} all-gather(f32[1,4,1024]{2,1,0:T(4,128)S(1)} %maximum_bitcast_fusion), channel_id=3, replica_groups=mesh['dp'=1,'tp'=4,'ep'=8] {'ep','tp'}, dimensions={0}, use_global_device_ids=true | all-gather | bytes 540672 | tf_op jit(solution)/shard_map/all_gather | solution.py:498
  57.7 0.1 pad.3.clone
  57.7 0.1 maximum_maximum_fusion
  57.8 1.0 copy.31.col_ref
  58.8 0.6 pad_add_fusion.pos_ref
  59.4 108.3 %all-gather.13.cloned.1.call-done = bf16[32768,768]{1,0:T(8,128)(2,1)} async-done(((bf16[1024,768]{1,0:T(8,128)(2,1)}), bf16[32768,768]{1,0:T(8,128)(2,1)}) %all-gather.13.cloned.1.call-update) | async-done | bytes 50331664 | tf_op jit(solution)/shard_map/all_gather | solution.py:490
  167.7 78.7 %hidden_rows.1 = (bf16[16,2,512,768]{3,2,1,0:T(8,128)(2,1)}, f32[16,2,512,768]{3,2,1,0:T(8,128)}, f32[16,2,512,768]{3,2,1,0:T(8,128)}) custom-call(s32[3]{0:T(128)} %pad_add_fusion.pos_ref, bf16[32,1024,768]{2,1,0:T(8,128)(2,1)} %bitcast.51, f32[32,4,1024]{2,1,0:T(4,128)} %all-gather.5.meta_ref, bf16[2,768,768]{2,1,0:T(8,128)(2,1)} %w1_ref.1, ...), custom_call_target="tpu_custom_call" | custom-call | flops 64424509440 | bytes 150994944 | tf_op jit(solution)/shard_map/hidden_rows/pallas_call | solution.py:89
  246.4 74.7 %all-gather.11.cloned.1.call-done = bf16[32768,768]{1,0:T(8,128)(2,1)} async-done(((bf16[1024,768]{1,0:T(8,128)(2,1)}), bf16[32768,768]{1,0:T(8,128)(2,1)}) %all-gather.11.cloned.1.call-update) | async-done | bytes 50331664 | tf_op jit(solution)/shard_map/all_gather | solution.py:491
  321.1 131.9 %weight_grads.1 = (bf16[2,768,768]{2,1,0:T(8,128)(2,1)}, bf16[2,768,768]{2,1,0:T(8,128)(2,1)}, bf16[2,768,768]{2,1,0:T(8,128)(2,1)}, bf16[8,2,256,768]{3,2,1,0:T(8,128)(2,1)}, bf16[8,2,256,768]{3,2,1,0:T(8,128)(2,1)}) custom-call(s32[3]{0:T(128)} %pad_add_fusion.pos_ref, bf16[32,1024,768]{2,1,0:T(8,128)(2,1)} %bitcast.50, ...), custom_call_target="tpu_custom_call" | custom-call | flops 103079215104 | bytes 150994944 | tf_op jit(solution)/shard_map/weight_grads/pallas_call | solution.py:192
  453.0 93.2 %own_rows.3.home1_ref = bf16[8,2,256,768]{3,2,1,0:T(8,128)(2,1)} custom-call(bf16[8,2,256,768]{3,2,1,0:T(8,128)(2,1)} %get-tuple-element.20.x_ref, bf16[8,2,256,768]{3,2,1,0:T(8,128)(2,1)} %get-tuple-element.21.g_ref, bf16[4,3,768,768]{3,2,1,0:T(8,128)(2,1)} %bitcast.52), custom_call_target="tpu_custom_call" | custom-call | flops 57982058496 | bytes 26738688 | tf_op jit(solution)/shard_map/own_rows/pallas_call | solution.py:334
  546.2 37.3 %all-gather.15.cloned.1.call-done = bf16[12,768,768]{2,1,0:T(8,128)(2,1)} async-done(((bf16[3,768,768]{2,1,0:T(8,128)(2,1)}), bf16[12,768,768]{2,1,0:T(8,128)(2,1)}) %all-gather.15.cloned.1.call-update) | async-done | bytes 14155792 | tf_op jit(solution)/shard_map/all_gather | solution.py:493
  583.5 93.5 %own_rows.2.home0_ref = bf16[8,2,256,768]{3,2,1,0:T(8,128)(2,1)} custom-call(bf16[8,2,256,768]{3,2,1,0:T(8,128)(2,1)} %get-tuple-element.20.x_ref, bf16[8,2,256,768]{3,2,1,0:T(8,128)(2,1)} %get-tuple-element.21.g_ref, bf16[4,3,768,768]{3,2,1,0:T(8,128)(2,1)} %bitcast.53), custom_call_target="tpu_custom_call" | custom-call | flops 57982058496 | bytes 26738688 | tf_op jit(solution)/shard_map/own_rows/pallas_call | solution.py:334
  677.0 32.0 %combine.1 = (bf16[1024,768]{1,0:T(8,128)(2,1)}, bf16[1024,768]{1,0:T(8,128)(2,1)}, f32[16,768]{1,0:T(8,128)}) custom-call(bf16[8,2,256,768]{3,2,1,0:T(8,128)(2,1)} %own_rows.2.home0_ref, bf16[8,2,256,768]{3,2,1,0:T(8,128)(2,1)} %own_rows.3.home1_ref, f32[1024,8]{1,0:T(8,128)} %copy.31.col_ref, bf16[1024,768]{1,0:T(8,128)(2,1)} %tok_ref.1, ...), custom_call_target="tpu_custom_call" | custom-call | flops 19327352832 | bytes 12582912 | tf_op jit(solution)/shard_map/combine/pallas_call | solution.py:408
  709.0 15.7 %router_sum.1 = f32[16,768]{1,0:T(8,128)} custom-call(f32[16,768]{1,0:T(8,128)} %get-tuple-element.27.part_ref), custom_call_target="tpu_custom_call" | custom-call | flops 147456 | bytes 98304 | tf_op jit(solution)/shard_map/router_sum/pallas_call | solution.py:461
  724.8 1.4 copy.38
  (26 shorter events, 0.4 us)
Async XLA Ops:
  7.2 1.7 copy-start.1
  7.2 160.5 %all-gather.13.cloned.1.call-start = ((), (), s32[]{:S(2)}) async-start(), calls=%async_computation.1 | async-start | bytes 51904512 | tf_op jit(solution)/shard_map/all_gather | solution.py:490
  8.0 313.1 %all-gather.11.cloned.1.call-start = ((), (), s32[]{:S(2)}) async-start(), calls=%async_computation | async-start | bytes 51904512 | tf_op jit(solution)/shard_map/all_gather | solution.py:491
  8.8 444.2 %all-gather.17.cloned.1.call-start = ((), (), s32[]{:S(2)}) async-start(), calls=%async_computation.3 | async-start | bytes 17694720 | tf_op jit(solution)/shard_map/all_gather | solution.py:493
  8.9 1.7 copy-start.2
  8.9 2.4 copy-start.3
  13.7 569.9 %all-gather.15.cloned.1.call-start = ((), (), s32[]{:S(2)}) async-start(), calls=%async_computation.2 | async-start | bytes 17694720 | tf_op jit(solution)/shard_map/all_gather | solution.py:493
  15.7 1.4 copy-start
  15.7 1.4 copy-start.5
  15.7 1.9 copy-start.4
Sparse Core Ops, SparseCore 0:
  10.2 157.4 all-gather.12
  169.8 151.2 all-gather.10
  322.7 128.4 all-gather.16
  452.6 130.9 all-gather.14
